TPU v7x, 32 devices: a whole 2x2x4 slice. The times are simulated.
32 devices in a mesh: dom: 8 (over z, y), ray: 4 (over x, core).
Axes of the slice: x: 2, y: 2, z: 4, core: 2. Of those that a mesh axis runs over, the one named last changes fastest.
Arguments:
- projections: bfloat16 [8, 64, 8192], P('dom', None, 'ray'), may hold values from -6 to 6
- phase_kernel: bfloat16 [129], replicated, may hold values from -0.5 to 0.5
- image: bfloat16 [16384, 64], P('dom'), may hold values from -6 to 6
- tile_library: bfloat16 [8, 4, 16, 128, 128], P('dom', 'ray'), may hold values from -0.09375 to 0.09375
- tile_entry: int32 [8, 4, 256], P('dom', 'ray'), may hold values from 0 to 15
- tile_image: int32 [8, 4, 256], P('dom', 'ray'), may hold values from 0 to 15
- tile_slot: int32 [8, 4, 256], P('dom', 'ray'), may hold values from 0 to 7
- tile_count: int32 [8, 4], P('dom', 'ray'), may hold values from 64 to 256, as said below
- slot_block: int32 [8, 4, 8], P('dom', 'ray'), may hold values from 0 to 15
Outputs:
- residual: bfloat16 [8, 64, 8192], P('dom', None, 'ray')
- image_next: float32 [16384, 64], P(('dom', 'ray'))
Inputs may be any that keep to these rules, and one draw needn't show every extreme that they name: `tile_count`: each device has at most 256 live tiles; some device holds exactly 256. Entries beyond a device's count are not used.
All inputs are finite; a program needn't handle non-finite values.
Results may differ from a plain program's by a relative error of at most 0.0075.
Values may be sent and summed in bfloat16 or wider, within the bound.
A program may use at most 64 MiB of HBM per device.

v0:
```python
import jax
import jax.numpy as jnp
from jax import lax
from jax.sharding import PartitionSpec as P

SMOOTH = 8
relax_factor = 0.25


def with_halo(cells, sides, width):
    for axis, dim in sides:
        count = lax.axis_size(axis)
        ends = count - 1
        head = lax.slice_in_dim(cells, 0, width, axis=dim)
        tail = lax.slice_in_dim(cells, cells.shape[dim] - width, cells.shape[dim], axis=dim)
        cells = jnp.concatenate(
            [
                lax.ppermute(tail, axis, [(i, (i + 1) % count) for i in range(ends)]),
                cells,
                lax.ppermute(head, axis, [((i + 1) % count, i) for i in range(ends)]),
            ],
            axis=dim,
        )
    return cells


def toeplitz(kernel, tile_size):
    taps = kernel.shape[0]
    padded = jnp.concatenate([kernel, jnp.zeros((2 * tile_size + 1 - taps,), kernel.dtype)])
    tiled = jnp.tile(padded, tile_size)[: 2 * tile_size * tile_size]
    return tiled.reshape(tile_size, 2 * tile_size).T


def phase_filter(projections, phase_kernel, tile_size):
    half_width = (phase_kernel.shape[0] - 1) // 2
    angles, slices, columns = projections.shape
    block_count = columns // tile_size
    rimmed = with_halo(projections, (("ray", 2),), half_width)
    padded = jnp.pad(rimmed, ((0, 0), (0, 0), (0, 2 * tile_size - 2 * half_width)))
    blocks = padded.reshape(angles, slices, block_count + 2, tile_size)
    windows = jnp.concatenate(
        [blocks[:, :, :block_count], blocks[:, :, 1 : block_count + 1]], axis=-1
    )
    filtered = jnp.einsum(
        "asbi,ij->asbj",
        windows,
        toeplitz(phase_kernel, tile_size),
        preferred_element_type=jnp.float32,
    )
    return filtered.reshape(angles, slices, columns).astype(jnp.bfloat16)


def stripe_profile(gathered):
    profile = jnp.median(gathered.astype(jnp.float32), axis=0)
    columns = profile.shape[1]
    rimmed = with_halo(profile, (("ray", 1),), SMOOTH)
    window_sum = jnp.zeros_like(profile)
    for offset in range(2 * SMOOTH + 1):
        window_sum = window_sum + rimmed[:, offset : offset + columns]
    position = lax.axis_index("ray") * columns + jnp.arange(columns)
    detector = lax.axis_size("ray") * columns
    in_range = (
        jnp.minimum(position + SMOOTH, detector - 1) - jnp.maximum(position - SMOOTH, 0) + 1
    ).astype(jnp.float32)
    return (profile - window_sum / in_range).astype(jnp.bfloat16)


def shards(
    projections,
    phase_kernel,
    image,
    tile_library,
    tile_entry,
    tile_image,
    tile_slot,
    tile_count,
    slot_block,
):
    tile_size = tile_library.shape[-1]
    angles, slices, columns = projections.shape
    phase = phase_filter(projections, phase_kernel, tile_size)
    gathered = lax.all_to_all(phase, "dom", split_axis=1, concat_axis=0, tiled=True)
    stripe = stripe_profile(gathered)
    fixed_rows = (gathered.astype(jnp.float32) - stripe.astype(jnp.float32)[None]).astype(
        jnp.bfloat16
    )
    corrected = lax.all_to_all(fixed_rows, "dom", split_axis=0, concat_axis=1, tiled=True)
    owners = lax.axis_size("dom")
    library = tile_library[0, 0]
    entries = tile_entry[0, 0]
    images = tile_image[0, 0]
    slots = tile_slot[0, 0]
    capacity = entries.shape[0]
    block_size = 64
    turn_count = capacity // block_size
    image_blocks = image.reshape(-1, tile_size, slices)
    block_total = image_blocks.shape[0]
    live_mask = jnp.arange(capacity) < tile_count[0, 0]
    slot_target = jnp.where(live_mask, slots, owners)
    image_target = jnp.where(live_mask, images, block_total)

    def forward_turn(turn_index, partial_value):
        first_tile = turn_index * block_size
        chosen = lax.dynamic_slice_in_dim(entries, first_tile, block_size)
        placed = lax.dynamic_slice_in_dim(images, first_tile, block_size)
        destined = lax.dynamic_slice_in_dim(slot_target, first_tile, block_size)
        product = jnp.einsum(
            "krp,kps->ksr",
            library[chosen],
            image_blocks[placed],
            preferred_element_type=jnp.float32,
        )
        return partial_value.at[destined].add(product, mode="drop")

    partial_value = lax.fori_loop(
        0, turn_count, forward_turn, jnp.zeros((owners, slices, tile_size), jnp.float32)
    )
    received = lax.all_to_all(
        partial_value.astype(jnp.bfloat16), "dom", split_axis=0, concat_axis=0, tiled=True
    )
    per_owner = columns // tile_size
    carried = slot_block[0, 0]
    block_ids = jnp.arange(angles * per_owner).reshape(angles, per_owner)
    selector = (block_ids[:, :, None] == carried[None, None, :]).astype(jnp.bfloat16)
    forward = jnp.einsum("abd,dst->asbt", selector, received, preferred_element_type=jnp.float32)
    residual = (corrected.astype(jnp.float32) - forward.reshape(angles, slices, columns)).astype(
        jnp.bfloat16
    )
    back = jnp.einsum(
        "abd,asbt->dst",
        selector,
        residual.reshape(angles, slices, per_owner, tile_size),
        preferred_element_type=jnp.float32,
    ).astype(jnp.bfloat16)
    returned = lax.all_to_all(back, "dom", split_axis=0, concat_axis=0, tiled=True)

    def adjoint_turn(turn_index, gradient):
        first_tile = turn_index * block_size
        chosen = lax.dynamic_slice_in_dim(entries, first_tile, block_size)
        sourced = lax.dynamic_slice_in_dim(slots, first_tile, block_size)
        destined = lax.dynamic_slice_in_dim(image_target, first_tile, block_size)
        product = jnp.einsum(
            "krp,ksr->kps", library[chosen], returned[sourced], preferred_element_type=jnp.float32
        )
        return gradient.at[destined].add(product, mode="drop")

    gradient = lax.fori_loop(
        0, turn_count, adjoint_turn, jnp.zeros((block_total, tile_size, slices), jnp.float32)
    )
    gradient = gradient.reshape(-1, slices)
    rows_own = gradient.shape[0] // lax.axis_size("ray")
    update = lax.psum_scatter(gradient, "ray", scatter_dimension=0, tiled=True)
    own_image = lax.dynamic_slice_in_dim(image, lax.axis_index("ray") * rows_own, rows_own)
    image_next = own_image.astype(jnp.float32) + relax_factor * update
    return (residual, image_next)


def solution(mesh):
    return jax.shard_map(
        shards,
        mesh=mesh,
        in_specs=(
            P("dom", None, "ray"),
            P(),
            P("dom", None),
            P("dom", "ray", None, None, None),
            P("dom", "ray", None),
            P("dom", "ray", None),
            P("dom", "ray", None),
            P("dom", "ray"),
            P("dom", "ray", None),
        ),
        out_specs=(P("dom", None, "ray"), P(("dom", "ray"), None)),
        check_vma=False,
    )
```

profile of v0, /device:TPU:0, one launch (start us, length us, event | category | flops | bytes accessed | tf_op | source)
XLA Modules:
  0.0 196.1 jit_solution(8649035580683881368)
XLA Ops:
  8.0 2.4 %collective-permute-start = (bf16[1,64,64]{2,1,0:T(8,128)(2,1)S(1)}, bf16[1,64,64]{2,1,0:T(8,128)(2,1)S(1)}, u32[]{:S(2)}, u32[]{:S(2)}) collective-permute-start(bf16[1,64,64]{2,1,0:T(8,128)(2,1)S(1)} %get-tuple-element.333), channel_id=1, source_target_pairs={{0,1},{1,2},{2,3},{4,5},{5,6},{6,7},{8,9},{9,10},{10,11},{12,13},{... | collective-permute-start | bytes 24584 | tf_op jit(solution)/shard_map/ppermute | solution.py:18
  10.4 1.3 collective-permute-start.1
  18.1 2.2 %reduce = bf16[64,2048]{1,0:T(8,128)(2,1)S(1)} reduce(bf16[64,1,2048]{2,1,0:T(2,128)(2,1)S(1)} %bitcast.81, bf16[]{:T(256)} %broadcast.188), dimensions={1}, to_apply=%bitcast.54.reduce_sub_computation | reduce | bytes 524290
  21.2 6.4 %all-to-all-start = ((bf16[8,2,8192]{2,1,0:T(2,128)(2,1)}), bf16[8,2,8192]{2,1,0:T(2,128)(2,1)}, u32[]{:S(2)}, u32[]{:S(2)}) async-start(bf16[8,2,8192]{2,1,0:T(2,128)(2,1)} %reshape.296), calls=%async_computation | async-start | bytes 524288 | tf_op jit(solution)/shard_map/all_to_all | solution.py:82
  27.7 47.9 %while.28 = (s32[]{:T(128)}, f32[8,64,128]{2,1,0:T(8,128)S(1)}, s32[256]{0:T(256)S(1)}, s32[256]{0:T(256)S(1)}, bf16[16,128,64]{2,1,0:T(8,128)(2,1)S(1)}, /*inde...) while((s32[]{:T(128)}, f32[8,64,128]{2,1,0:T(8,128)S(1)}, ...), condition=%wide.region_4.5_spmd, body=%wide.region_2.4_spmd.sunk | while | flops 134744640 | bytes 17836972 | solution.py:115
  27.9 2.2 %gather_fusion = bf16[64,128,64]{2,1,0:T(8,128)(2,1)} fusion(bf16[16,128,64]{2,1,0:T(8,128)(2,1)S(1)} %get-tuple-element.456, s32[1024]{0:T(1024)S(1)} %pad_clamp_fusion.8), kind=kCustom, calls=%fused_computation.clone.1 | custom fusion | bytes 2097408 | tf_op jit(solution)/shard_map/while/body/eval_jaxpr/gather | solution.py:110
  30.1 2.1 %gather_fusion.1 = bf16[64,128,128]{2,1,0:T(8,128)(2,1)} fusion(bf16[16,128,128]{2,1,0:T(8,128)(2,1)S(1)} %get-tuple-element.458, s32[1024]{0:T(1024)S(1)} %pad_clamp_fusion.9), kind=kCustom, calls=%fused_computation.1.clone.1 | custom fusion | bytes 4194560 | tf_op jit(solution)/shard_map/while/body/eval_jaxpr/gather | solution.py:109
  32.2 3.7 %fusion.71 = f32[64,64,128]{2,1,0:T(8,128)S(1)} fusion(bf16[64,128,64]{2,1,0:T(8,128)(2,1)} %gather_fusion, bf16[64,128,128]{2,1,0:T(8,128)(2,1)} %gather_fusion.1), kind=kOutput, calls=%fused_computation.113.clone.1 | convolution fusion | flops 134217728 | bytes 5242880 | tf_op jit(solution)/shard_map/while/body/eval_jaxpr/krp,kps->ksr/dot_general | solution.py:107
  35.9 3.8 %scatter_fusion = f32[8,64,128]{2,1,0:T(8,128)S(1)} fusion(f32[8,64,128]{2,1,0:T(8,128)S(1)} %get-tuple-element.442, s32[64]{0:T(128)S(1)} %compare_select_fusion.10, f32[64,64,128]{2,1,0:T(8,128)S(1)} %fusion.71), kind=kCustom, calls=%fused_computation.4.clone.1 | custom fusion | flops 524288 | bytes 6291712 | tf_op jit(solution)/shard_map/while/body/eval_jaxpr/scatter-add | solution.py:113
  39.9 2.2 %gather_fusion = bf16[64,128,64]{2,1,0:T(8,128)(2,1)} fusion(bf16[16,128,64]{2,1,0:T(8,128)(2,1)S(1)} %get-tuple-element.456, s32[1024]{0:T(1024)S(1)} %pad_clamp_fusion.8), kind=kCustom, calls=%fused_computation.clone.1 | custom fusion | bytes 2097408 | tf_op jit(solution)/shard_map/while/body/eval_jaxpr/gather | solution.py:110
  42.0 2.1 %gather_fusion.1 = bf16[64,128,128]{2,1,0:T(8,128)(2,1)} fusion(bf16[16,128,128]{2,1,0:T(8,128)(2,1)S(1)} %get-tuple-element.458, s32[1024]{0:T(1024)S(1)} %pad_clamp_fusion.9), kind=kCustom, calls=%fused_computation.1.clone.1 | custom fusion | bytes 4194560 | tf_op jit(solution)/shard_map/while/body/eval_jaxpr/gather | solution.py:109
  44.1 3.7 %fusion.71 = f32[64,64,128]{2,1,0:T(8,128)S(1)} fusion(bf16[64,128,64]{2,1,0:T(8,128)(2,1)} %gather_fusion, bf16[64,128,128]{2,1,0:T(8,128)(2,1)} %gather_fusion.1), kind=kOutput, calls=%fused_computation.113.clone.1 | convolution fusion | flops 134217728 | bytes 5242880 | tf_op jit(solution)/shard_map/while/body/eval_jaxpr/krp,kps->ksr/dot_general | solution.py:107
  47.9 3.8 %scatter_fusion = f32[8,64,128]{2,1,0:T(8,128)S(1)} fusion(f32[8,64,128]{2,1,0:T(8,128)S(1)} %get-tuple-element.442, s32[64]{0:T(128)S(1)} %compare_select_fusion.10, f32[64,64,128]{2,1,0:T(8,128)S(1)} %fusion.71), kind=kCustom, calls=%fused_computation.4.clone.1 | custom fusion | flops 524288 | bytes 6291712 | tf_op jit(solution)/shard_map/while/body/eval_jaxpr/scatter-add | solution.py:113
  51.8 2.2 %gather_fusion = bf16[64,128,64]{2,1,0:T(8,128)(2,1)} fusion(bf16[16,128,64]{2,1,0:T(8,128)(2,1)S(1)} %get-tuple-element.456, s32[1024]{0:T(1024)S(1)} %pad_clamp_fusion.8), kind=kCustom, calls=%fused_computation.clone.1 | custom fusion | bytes 2097408 | tf_op jit(solution)/shard_map/while/body/eval_jaxpr/gather | solution.py:110
  54.0 2.1 %gather_fusion.1 = bf16[64,128,128]{2,1,0:T(8,128)(2,1)} fusion(bf16[16,128,128]{2,1,0:T(8,128)(2,1)S(1)} %get-tuple-element.458, s32[1024]{0:T(1024)S(1)} %pad_clamp_fusion.9), kind=kCustom, calls=%fused_computation.1.clone.1 | custom fusion | bytes 4194560 | tf_op jit(solution)/shard_map/while/body/eval_jaxpr/gather | solution.py:109
  56.1 3.7 %fusion.71 = f32[64,64,128]{2,1,0:T(8,128)S(1)} fusion(bf16[64,128,64]{2,1,0:T(8,128)(2,1)} %gather_fusion, bf16[64,128,128]{2,1,0:T(8,128)(2,1)} %gather_fusion.1), kind=kOutput, calls=%fused_computation.113.clone.1 | convolution fusion | flops 134217728 | bytes 5242880 | tf_op jit(solution)/shard_map/while/body/eval_jaxpr/krp,kps->ksr/dot_general | solution.py:107
  59.9 3.8 %scatter_fusion = f32[8,64,128]{2,1,0:T(8,128)S(1)} fusion(f32[8,64,128]{2,1,0:T(8,128)S(1)} %get-tuple-element.442, s32[64]{0:T(128)S(1)} %compare_select_fusion.10, f32[64,64,128]{2,1,0:T(8,128)S(1)} %fusion.71), kind=kCustom, calls=%fused_computation.4.clone.1 | custom fusion | flops 524288 | bytes 6291712 | tf_op jit(solution)/shard_map/while/body/eval_jaxpr/scatter-add | solution.py:113
  63.8 2.2 %gather_fusion = bf16[64,128,64]{2,1,0:T(8,128)(2,1)} fusion(bf16[16,128,64]{2,1,0:T(8,128)(2,1)S(1)} %get-tuple-element.456, s32[1024]{0:T(1024)S(1)} %pad_clamp_fusion.8), kind=kCustom, calls=%fused_computation.clone.1 | custom fusion | bytes 2097408 | tf_op jit(solution)/shard_map/while/body/eval_jaxpr/gather | solution.py:110
  66.0 2.1 %gather_fusion.1 = bf16[64,128,128]{2,1,0:T(8,128)(2,1)} fusion(bf16[16,128,128]{2,1,0:T(8,128)(2,1)S(1)} %get-tuple-element.458, s32[1024]{0:T(1024)S(1)} %pad_clamp_fusion.9), kind=kCustom, calls=%fused_computation.1.clone.1 | custom fusion | bytes 4194560 | tf_op jit(solution)/shard_map/while/body/eval_jaxpr/gather | solution.py:109
  68.1 3.7 %fusion.71 = f32[64,64,128]{2,1,0:T(8,128)S(1)} fusion(bf16[64,128,64]{2,1,0:T(8,128)(2,1)} %gather_fusion, bf16[64,128,128]{2,1,0:T(8,128)(2,1)} %gather_fusion.1), kind=kOutput, calls=%fused_computation.113.clone.1 | convolution fusion | flops 134217728 | bytes 5242880 | tf_op jit(solution)/shard_map/while/body/eval_jaxpr/krp,kps->ksr/dot_general | solution.py:107
  71.8 3.8 %scatter_fusion = f32[8,64,128]{2,1,0:T(8,128)S(1)} fusion(f32[8,64,128]{2,1,0:T(8,128)S(1)} %get-tuple-element.442, s32[64]{0:T(128)S(1)} %compare_select_fusion.10, f32[64,64,128]{2,1,0:T(8,128)S(1)} %fusion.71), kind=kCustom, calls=%fused_computation.4.clone.1 | custom fusion | flops 524288 | bytes 6291712 | tf_op jit(solution)/shard_map/while/body/eval_jaxpr/scatter-add | solution.py:113
  76.3 6.0 %all-to-all-start.2 = ((bf16[8,64,128]{2,1,0:T(8,128)(2,1)}), bf16[8,64,128]{2,1,0:T(8,128)(2,1)S(1)}, u32[]{:S(2)}, u32[]{:S(2)}) async-start(bf16[8,64,128]{2,1,0:T(8,128)(2,1)} %convert_element_type.108), calls=%async_computation.2 | async-start | bytes 262144 | tf_op jit(solution)/shard_map/all_to_all | solution.py:118
  84.2 4.8 %sort.16 = (f32[8,8,2048]{2,0,1:T(8,128)S(1)}, s32[8,8,2048]{2,0,1:T(8,128)}) sort(f32[8,8,2048]{2,0,1:T(8,128)S(1)} %copy_select_fusion, s32[8,8,2048]{2,0,1:T(8,128)S(1)} %iota.19), dimensions={0}, to_apply=%region_1.2 | sort | flops 2228224 | bytes 2097152 | tf_op jit(solution)/shard_map/jit(median)/jit(quantile)/sort | solution.py:54
  89.2 1.3 collective-permute-start.3
  90.5 4.1 %collective-permute-start.2 = (f32[8,8]{1,0:T(8,128)S(1)}, f32[8,8]{1,0:T(8,128)S(1)}, u32[]{:S(2)}, u32[]{:S(2)}) collective-permute-start(f32[8,8]{1,0:T(8,128)S(1)} %get-tuple-element.334), channel_id=1, source_target_pairs={{0,1},{1,2},{2,3},{4,5},{5,6},{6,7},{8,9},{9,10},{10,11},{12,13},{... | collective-permute-start | bytes 776 | tf_op jit(solution)/shard_map/ppermute | solution.py:18
  96.6 5.7 %all-to-all-start.1 = ((bf16[8,8,2048]{2,1,0:T(8,128)(2,1)}), bf16[8,8,2048]{2,1,0:T(8,128)(2,1)S(1)}, u32[]{:S(2)}, u32[]{:S(2)}) async-start(bf16[8,8,2048]{2,1,0:T(8,128)(2,1)} %subtract_convert_fusion), calls=%async_computation.1 | async-start | bytes 524288 | tf_op jit(solution)/shard_map/all_to_all | solution.py:87
  102.7 8.1 %all-to-all-done.1 = bf16[8,8,2048]{2,1,0:T(8,128)(2,1)S(1)} async-done(((bf16[8,8,2048]{2,1,0:T(8,128)(2,1)}), bf16[8,8,2048]{2,1,0:T(8,128)(2,1)S(1)}, u32[]{:S(2)}, u32[]{:S(2)}) %all-to-all-start.1) | async-done | bytes 262176 | tf_op jit(solution)/shard_map/all_to_all | solution.py:87
  111.8 5.0 %all-to-all-start.3 = ((bf16[8,64,128]{2,1,0:T(8,128)(2,1)}), bf16[8,64,128]{2,1,0:T(8,128)(2,1)S(1)}, u32[]{:S(2)}, u32[]{:S(2)}) async-start(bf16[8,64,128]{2,1,0:T(8,128)(2,1)} %copy.34), calls=%async_computation.3 | async-start | bytes 262144 | tf_op jit(solution)/shard_map/all_to_all | solution.py:135
  116.9 7.4 %all-to-all-done.3 = bf16[8,64,128]{2,1,0:T(8,128)(2,1)S(1)} async-done(((bf16[8,64,128]{2,1,0:T(8,128)(2,1)}), bf16[8,64,128]{2,1,0:T(8,128)(2,1)S(1)}, u32[]{:S(2)}, u32[]{:S(2)}) %all-to-all-start.3) | async-done | bytes 131104 | tf_op jit(solution)/shard_map/all_to_all | solution.py:135
  124.3 41.5 %while.29 = (s32[]{:T(128)}, f32[16,128,64]{1,2,0:T(8,128)S(1)}, s32[256]{0:T(256)S(1)}, s32[256]{0:T(256)S(1)}, bf16[16,128,128]{2,1,0:T(8,128)(2,1)S(1)}, /*in...) while((s32[]{:T(128)}, f32[16,128,64]{1,2,0:T(8,128)S(1)}, ...), condition=%wide.region_7.8_spmd, body=%wide.region_5.7_spmd.sunk | while | flops 134744640 | bytes 17836972 | solution.py:147
  124.5 1.7 gather_fusion.2
  126.2 2.2 %gather_fusion.3 = bf16[64,128,128]{2,1,0:T(8,128)(2,1)} fusion(bf16[16,128,128]{2,1,0:T(8,128)(2,1)S(1)} %get-tuple-element.489, s32[1024]{0:T(1024)S(1)} %pad_clamp_fusion.11), kind=kCustom, calls=%fused_computation.2.clone.1 | custom fusion | bytes 4194560 | tf_op jit(solution)/shard_map/while/body/eval_jaxpr/gather | solution.py:143
  128.4 2.6 %fusion.74 = f32[64,128,64]{1,2,0:T(8,128)S(1)} fusion(bf16[64,64,128]{2,1,0:T(8,128)(2,1)} %gather_fusion.2, bf16[64,128,128]{2,1,0:T(8,128)(2,1)} %gather_fusion.3), kind=kOutput, calls=%fused_computation.114.clone.1 | convolution fusion | flops 134217728 | bytes 5242880 | tf_op jit(solution)/shard_map/while/body/eval_jaxpr/krp,ksr->kps/dot_general | solution.py:142
  131.0 3.7 %scatter_fusion.1 = f32[16,128,64]{1,2,0:T(8,128)S(1)} fusion(f32[16,128,64]{1,2,0:T(8,128)S(1)} %get-tuple-element.475, s32[64]{0:T(128)S(1)} %compare_select_fusion.12, f32[64,128,64]{1,2,0:T(8,128)S(1)} %fusion.74), kind=kCustom, calls=%fused_computation.5.clone.1 | custom fusion | flops 524288 | bytes 6291712 | tf_op jit(solution)/shard_map/while/body/eval_jaxpr/scatter-add | solution.py:145
  134.9 1.7 gather_fusion.2
  136.5 2.2 %gather_fusion.3 = bf16[64,128,128]{2,1,0:T(8,128)(2,1)} fusion(bf16[16,128,128]{2,1,0:T(8,128)(2,1)S(1)} %get-tuple-element.489, s32[1024]{0:T(1024)S(1)} %pad_clamp_fusion.11), kind=kCustom, calls=%fused_computation.2.clone.1 | custom fusion | bytes 4194560 | tf_op jit(solution)/shard_map/while/body/eval_jaxpr/gather | solution.py:143
  138.7 2.6 %fusion.74 = f32[64,128,64]{1,2,0:T(8,128)S(1)} fusion(bf16[64,64,128]{2,1,0:T(8,128)(2,1)} %gather_fusion.2, bf16[64,128,128]{2,1,0:T(8,128)(2,1)} %gather_fusion.3), kind=kOutput, calls=%fused_computation.114.clone.1 | convolution fusion | flops 134217728 | bytes 5242880 | tf_op jit(solution)/shard_map/while/body/eval_jaxpr/krp,ksr->kps/dot_general | solution.py:142
  141.3 3.8 %scatter_fusion.1 = f32[16,128,64]{1,2,0:T(8,128)S(1)} fusion(f32[16,128,64]{1,2,0:T(8,128)S(1)} %get-tuple-element.475, s32[64]{0:T(128)S(1)} %compare_select_fusion.12, f32[64,128,64]{1,2,0:T(8,128)S(1)} %fusion.74), kind=kCustom, calls=%fused_computation.5.clone.1 | custom fusion | flops 524288 | bytes 6291712 | tf_op jit(solution)/shard_map/while/body/eval_jaxpr/scatter-add | solution.py:145
  145.3 1.7 gather_fusion.2
  146.9 2.2 %gather_fusion.3 = bf16[64,128,128]{2,1,0:T(8,128)(2,1)} fusion(bf16[16,128,128]{2,1,0:T(8,128)(2,1)S(1)} %get-tuple-element.489, s32[1024]{0:T(1024)S(1)} %pad_clamp_fusion.11), kind=kCustom, calls=%fused_computation.2.clone.1 | custom fusion | bytes 4194560 | tf_op jit(solution)/shard_map/while/body/eval_jaxpr/gather | solution.py:143
  149.1 2.6 %fusion.74 = f32[64,128,64]{1,2,0:T(8,128)S(1)} fusion(bf16[64,64,128]{2,1,0:T(8,128)(2,1)} %gather_fusion.2, bf16[64,128,128]{2,1,0:T(8,128)(2,1)} %gather_fusion.3), kind=kOutput, calls=%fused_computation.114.clone.1 | convolution fusion | flops 134217728 | bytes 5242880 | tf_op jit(solution)/shard_map/while/body/eval_jaxpr/krp,ksr->kps/dot_general | solution.py:142
  151.7 3.8 %scatter_fusion.1 = f32[16,128,64]{1,2,0:T(8,128)S(1)} fusion(f32[16,128,64]{1,2,0:T(8,128)S(1)} %get-tuple-element.475, s32[64]{0:T(128)S(1)} %compare_select_fusion.12, f32[64,128,64]{1,2,0:T(8,128)S(1)} %fusion.74), kind=kCustom, calls=%fused_computation.5.clone.1 | custom fusion | flops 524288 | bytes 6291712 | tf_op jit(solution)/shard_map/while/body/eval_jaxpr/scatter-add | solution.py:145
  155.6 1.7 gather_fusion.2
  157.3 2.2 %gather_fusion.3 = bf16[64,128,128]{2,1,0:T(8,128)(2,1)} fusion(bf16[16,128,128]{2,1,0:T(8,128)(2,1)S(1)} %get-tuple-element.489, s32[1024]{0:T(1024)S(1)} %pad_clamp_fusion.11), kind=kCustom, calls=%fused_computation.2.clone.1 | custom fusion | bytes 4194560 | tf_op jit(solution)/shard_map/while/body/eval_jaxpr/gather | solution.py:143
  159.5 2.6 %fusion.74 = f32[64,128,64]{1,2,0:T(8,128)S(1)} fusion(bf16[64,64,128]{2,1,0:T(8,128)(2,1)} %gather_fusion.2, bf16[64,128,128]{2,1,0:T(8,128)(2,1)} %gather_fusion.3), kind=kOutput, calls=%fused_computation.114.clone.1 | convolution fusion | flops 134217728 | bytes 5242880 | tf_op jit(solution)/shard_map/while/body/eval_jaxpr/krp,ksr->kps/dot_general | solution.py:142
  162.1 3.8 %scatter_fusion.1 = f32[16,128,64]{1,2,0:T(8,128)S(1)} fusion(f32[16,128,64]{1,2,0:T(8,128)S(1)} %get-tuple-element.475, s32[64]{0:T(128)S(1)} %compare_select_fusion.12, f32[64,128,64]{1,2,0:T(8,128)S(1)} %fusion.74), kind=kCustom, calls=%fused_computation.5.clone.1 | custom fusion | flops 524288 | bytes 6291712 | tf_op jit(solution)/shard_map/while/body/eval_jaxpr/scatter-add | solution.py:145
  168.6 19.1 %reduce-scatter.2.cloned.1.call-done = f32[512,64]{0,1:T(8,128)} async-done(((f32[2048,64]{0,1:T(8,128)}), f32[512,64]{0,1:T(8,128)}) %reduce-scatter.2.cloned.1.call-update) | async-done | bytes 131088 | tf_op jit(solution)/shard_map/reduce_scatter | solution.py:152
  187.7 1.6 multiply_add_fusion
  (91 shorter events, 17.8 us)
Async XLA Ops:
  8.0 7.3 %collective-permute-start = (bf16[1,64,64]{2,1,0:T(8,128)(2,1)S(1)}, bf16[1,64,64]{2,1,0:T(8,128)(2,1)S(1)}, u32[]{:S(2)}, u32[]{:S(2)}) collective-permute-start(bf16[1,64,64]{2,1,0:T(8,128)(2,1)S(1)} %get-tuple-element.333), channel_id=1, source_target_pairs={{0,1},{1,2},{2,3},{4,5},{5,6},{6,7},{8,9},{9,10},{10,11},{12,13},{... | collective-permute-start | bytes 24584 | tf_op jit(solution)/shard_map/ppermute | solution.py:18
  10.4 5.2 %collective-permute-start.1 = (bf16[1,64,64]{2,1,0:T(8,128)(2,1)S(1)}, bf16[1,64,64]{2,1,0:T(8,128)(2,1)S(1)}, u32[]{:S(2)}, u32[]{:S(2)}) collective-permute-start(bf16[1,64,64]{2,1,0:T(8,128)(2,1)S(1)} %get-tuple-element.332), channel_id=1, source_target_pairs={{1,0},{2,1},{3,2},{5,4},{6,5},{7,6},{9,8},{10,9},{11,10},{13,12},{... | collective-permute-start | bytes 24584 | tf_op jit(solution)/shard_map/ppermute | solution.py:20
  17.1 10.6 %copy-start = (bf16[1,1,16,128,128]{4,3,2,1,0:T(8,128)(2,1)S(1)}, bf16[1,1,16,128,128]{4,3,2,1,0:T(8,128)(2,1)}, u32[]{:S(2)}) copy-start(bf16[1,1,16,128,128]{4,3,2,1,0:T(8,128)(2,1)} %param.16) | copy-start | bytes 1572868
  17.1 10.6 %copy-start.2 = (s32[1,1,256]{2,1,0:T(1,128)S(1)}, s32[1,1,256]{2,1,0:T(1,128)}, u32[]{:S(2)}) copy-start(s32[1,1,256]{2,1,0:T(1,128)} %param.17) | copy-start | bytes 3076
  17.1 10.6 %copy-start.3 = (s32[1,1,256]{2,1,0:T(1,128)S(1)}, s32[1,1,256]{2,1,0:T(1,128)}, u32[]{:S(2)}) copy-start(s32[1,1,256]{2,1,0:T(1,128)} %param.18) | copy-start | bytes 3076
  21.2 55.1 %all-to-all-start = ((bf16[8,2,8192]{2,1,0:T(2,128)(2,1)}), bf16[8,2,8192]{2,1,0:T(2,128)(2,1)}, u32[]{:S(2)}, u32[]{:S(2)}) async-start(bf16[8,2,8192]{2,1,0:T(2,128)(2,1)} %reshape.296), calls=%async_computation | async-start | bytes 524288 | tf_op jit(solution)/shard_map/all_to_all | solution.py:82
  76.3 20.3 %all-to-all-start.2 = ((bf16[8,64,128]{2,1,0:T(8,128)(2,1)}), bf16[8,64,128]{2,1,0:T(8,128)(2,1)S(1)}, u32[]{:S(2)}, u32[]{:S(2)}) async-start(bf16[8,64,128]{2,1,0:T(8,128)(2,1)} %convert_element_type.108), calls=%async_computation.2 | async-start | bytes 262144 | tf_op jit(solution)/shard_map/all_to_all | solution.py:118
  83.8 18.5 %copy-start.5 = (s32[1,1,8]{2,1,0:T(1,128)S(1)}, s32[1,1,8]{2,1,0:T(1,128)}, u32[]{:S(2)}) copy-start(s32[1,1,8]{2,1,0:T(1,128)} %param.21) | copy-start | bytes 100
  89.2 5.4 %collective-permute-start.3 = (f32[8,8]{1,0:T(8,128)S(1)}, f32[8,8]{1,0:T(8,128)S(1)}, u32[]{:S(2)}, u32[]{:S(2)}) collective-permute-start(f32[8,8]{1,0:T(8,128)S(1)} %get-tuple-element.335), channel_id=1, source_target_pairs={{1,0},{2,1},{3,2},{5,4},{6,5},{7,6},{9,8},{10,9},{11,10},{13,12},{... | collective-permute-start | bytes 776 | tf_op jit(solution)/shard_map/ppermute | solution.py:20
  90.5 4.9 %collective-permute-start.2 = (f32[8,8]{1,0:T(8,128)S(1)}, f32[8,8]{1,0:T(8,128)S(1)}, u32[]{:S(2)}, u32[]{:S(2)}) collective-permute-start(f32[8,8]{1,0:T(8,128)S(1)} %get-tuple-element.334), channel_id=1, source_target_pairs={{0,1},{1,2},{2,3},{4,5},{5,6},{6,7},{8,9},{9,10},{10,11},{12,13},{... | collective-permute-start | bytes 776 | tf_op jit(solution)/shard_map/ppermute | solution.py:18
  96.6 14.2 %all-to-all-start.1 = ((bf16[8,8,2048]{2,1,0:T(8,128)(2,1)}), bf16[8,8,2048]{2,1,0:T(8,128)(2,1)S(1)}, u32[]{:S(2)}, u32[]{:S(2)}) async-start(bf16[8,8,2048]{2,1,0:T(8,128)(2,1)} %subtract_convert_fusion), calls=%async_computation.1 | async-start | bytes 524288 | tf_op jit(solution)/shard_map/all_to_all | solution.py:87
  102.7 9.2 %copy-start.1 = (f32[1,64,16,128]{3,2,1,0:T(8,128)}, f32[1,64,16,128]{3,2,1,0:T(8,128)S(1)}, u32[]{:S(2)}) copy-start(f32[1,64,16,128]{3,2,1,0:T(8,128)S(1)} %convolution_bitcast_fusion) | copy-start | bytes 1572868
  102.7 21.7 %copy-start.4 = (s32[1,1,256]{2,1,0:T(1,128)S(1)}, s32[1,1,256]{2,1,0:T(1,128)}, u32[]{:S(2)}) copy-start(s32[1,1,256]{2,1,0:T(1,128)} %param.19) | copy-start | bytes 3076
  111.8 12.5 %all-to-all-start.3 = ((bf16[8,64,128]{2,1,0:T(8,128)(2,1)}), bf16[8,64,128]{2,1,0:T(8,128)(2,1)S(1)}, u32[]{:S(2)}, u32[]{:S(2)}) async-start(bf16[8,64,128]{2,1,0:T(8,128)(2,1)} %copy.34), calls=%async_computation.3 | async-start | bytes 262144 | tf_op jit(solution)/shard_map/all_to_all | solution.py:135
  116.8 70.9 %reduce-scatter.2.cloned.1.call-start = ((), (), s32[]{:S(2)}) async-start(), calls=%async_computation.5 | async-start | bytes 655360 | tf_op jit(solution)/shard_map/reduce_scatter | solution.py:152
Sparse Core Ops, SparseCore 0:
  166.8 20.8 reduce-scatter.1
where the time goes:
time: 197 us; the launch traced here: 196 us
  other arithmetic  44 us (22%)
  local copies, waits for them, and re-layouts  42.8 us (22%)
  waiting for transfers between devices  35.6 us (18%)
  starting transfers between devices  32.2 us (16%)
  matrix products  26.2 us (13%)
  between operations  15 us (8%)
    reduce_scatter x1, waiting for transfers between devices, shards(): update = lax.psum_scatter(gradient, 'ray', scatter_dimension=0, tiled=True)  19.1 us
    scatter-add x4, other arithmetic, forward_turn(): return partial_value.at[destined].add(product, mode='drop')  15 us
    scatter-add x4, other arithmetic, adjoint_turn(): return gradient.at[destined].add(product, mode='drop')  15 us
    dot_general x4, matrix products, forward_turn(): jnp.einsum('krp,kps->ksr', library[chosen], image_blocks[placed], preferr...  15 us
    dot_general x4, matrix products, adjoint_turn(): jnp.einsum('krp,ksr->kps', library[chosen], returned[sourced], preferred_...  10.4 us
    gather x4, local copies, waits for them, and re-layouts, forward_turn(): image_blocks[placed]  8.67 us
    gather x4, local copies, waits for them, and re-layouts, adjoint_turn(): library[chosen]  8.66 us
    gather x4, local copies, waits for them, and re-layouts, forward_turn(): library[chosen]  8.43 us
  transfers between devices with their start and end apart: 9, of which 5 were waited for; matrix products, arithmetic and copies ran while one was open for 31% of the time, Pallas kernels for 0%

commit v1 on v0

--- a/solution.py
+++ b/solution.py
@@ -84,7 +84,10 @@
     fixed_rows = (gathered.astype(jnp.float32) - stripe.astype(jnp.float32)[None]).astype(
         jnp.bfloat16
     )
-    corrected = lax.all_to_all(fixed_rows, "dom", split_axis=0, concat_axis=1, tiled=True)
+    size = lax.axis_size("dom")
+    pieces = jnp.stack(jnp.split(fixed_rows, size, axis=0), axis=0)
+    pieces = lax.all_to_all(pieces, "dom", split_axis=0, concat_axis=0)
+    corrected = jnp.concatenate(pieces, axis=1)
     owners = lax.axis_size("dom")
     library = tile_library[0, 0]
     entries = tile_entry[0, 0]

time: 197 us -> 201 us (1.020)
  local copies, waits for them, and re-layouts: 42.8 us -> 47.7 us
    unnamed x18 -> x25, local copies, waits for them, and re-layouts: 4.05 us -> 8.37 us
  transfers between devices with their start and end apart: 9 -> 9, of which waited for: 5 -> 5; matrix products, arithmetic and copies ran while one was open for 31% -> 33% of each run, Pallas kernels for 0% -> 0%
where the time goes in v1:
time: 201 us; the launch traced here: 200 us
  local copies, waits for them, and re-layouts  47.7 us (24%)
  other arithmetic  43.3 us (22%)
  waiting for transfers between devices  35.6 us (18%)
  starting transfers between devices  32.2 us (16%)
  matrix products  26.2 us (13%)
  between operations  15 us (7%)
    reduce_scatter x1, waiting for transfers between devices, shards(): update = lax.psum_scatter(gradient, 'ray', scatter_dimension=0, tiled=True)  19.1 us
    scatter-add x4, other arithmetic, forward_turn(): return partial_value.at[destined].add(product, mode='drop')  15 us
    scatter-add x4, other arithmetic, adjoint_turn(): return gradient.at[destined].add(product, mode='drop')  15 us
    dot_general x4, matrix products, forward_turn(): jnp.einsum('krp,kps->ksr', library[chosen], image_blocks[placed], preferr...  15 us
    dot_general x4, matrix products, adjoint_turn(): jnp.einsum('krp,ksr->kps', library[chosen], returned[sourced], preferred_...  10.4 us
    gather x4, local copies, waits for them, and re-layouts, forward_turn(): image_blocks[placed]  8.67 us
    gather x4, local copies, waits for them, and re-layouts, adjoint_turn(): library[chosen]  8.66 us
    gather x4, local copies, waits for them, and re-layouts, forward_turn(): library[chosen]  8.43 us
  transfers between devices with their start and end apart: 9, of which 5 were waited for; matrix products, arithmetic and copies ran while one was open for 33% of the time, Pallas kernels for 0%

profile of v1, /device:TPU:0, one launch (start us, length us, event | category | flops | bytes accessed | tf_op | source)
XLA Modules:
  0.0 200.4 jit_solution(6283780144326259690)
XLA Ops:
  8.0 2.4 %collective-permute-start = (bf16[1,64,64]{2,1,0:T(8,128)(2,1)S(1)}, bf16[1,64,64]{2,1,0:T(8,128)(2,1)S(1)}, u32[]{:S(2)}, u32[]{:S(2)}) collective-permute-start(bf16[1,64,64]{2,1,0:T(8,128)(2,1)S(1)} %get-tuple-element.333), channel_id=1, source_target_pairs={{0,1},{1,2},{2,3},{4,5},{5,6},{6,7},{8,9},{9,10},{10,11},{12,13},{... | collective-permute-start | bytes 24584 | tf_op jit(solution)/shard_map/ppermute | solution.py:18
  10.4 1.3 collective-permute-start.1
  18.1 2.2 %reduce = bf16[64,2048]{1,0:T(8,128)(2,1)S(1)} reduce(bf16[64,1,2048]{2,1,0:T(2,128)(2,1)S(1)} %bitcast.114, bf16[]{:T(256)} %broadcast.188), dimensions={1}, to_apply=%bitcast.87.reduce_sub_computation | reduce | bytes 524290
  21.2 6.4 %all-to-all-start = ((bf16[8,2,8192]{2,1,0:T(2,128)(2,1)}), bf16[8,2,8192]{2,1,0:T(2,128)(2,1)}, u32[]{:S(2)}, u32[]{:S(2)}) async-start(bf16[8,2,8192]{2,1,0:T(2,128)(2,1)} %reshape.293), calls=%async_computation | async-start | bytes 524288 | tf_op jit(solution)/shard_map/all_to_all | solution.py:82
  27.7 47.9 %while.28 = (s32[]{:T(128)}, f32[8,64,128]{2,1,0:T(8,128)S(1)}, s32[256]{0:T(256)S(1)}, s32[256]{0:T(256)S(1)}, bf16[16,128,64]{2,1,0:T(8,128)(2,1)S(1)}, /*inde...) while((s32[]{:T(128)}, f32[8,64,128]{2,1,0:T(8,128)S(1)}, ...), condition=%wide.region_4.5_spmd, body=%wide.region_2.4_spmd.sunk | while | flops 134744640 | bytes 17836972 | solution.py:118
  27.9 2.2 %gather_fusion = bf16[64,128,64]{2,1,0:T(8,128)(2,1)} fusion(bf16[16,128,64]{2,1,0:T(8,128)(2,1)S(1)} %get-tuple-element.456, s32[1024]{0:T(1024)S(1)} %pad_clamp_fusion.8), kind=kCustom, calls=%fused_computation.clone.1 | custom fusion | bytes 2097408 | tf_op jit(solution)/shard_map/while/body/eval_jaxpr/gather | solution.py:113
  30.1 2.1 %gather_fusion.1 = bf16[64,128,128]{2,1,0:T(8,128)(2,1)} fusion(bf16[16,128,128]{2,1,0:T(8,128)(2,1)S(1)} %get-tuple-element.458, s32[1024]{0:T(1024)S(1)} %pad_clamp_fusion.9), kind=kCustom, calls=%fused_computation.1.clone.1 | custom fusion | bytes 4194560 | tf_op jit(solution)/shard_map/while/body/eval_jaxpr/gather | solution.py:112
  32.2 3.7 %fusion.79 = f32[64,64,128]{2,1,0:T(8,128)S(1)} fusion(bf16[64,128,64]{2,1,0:T(8,128)(2,1)} %gather_fusion, bf16[64,128,128]{2,1,0:T(8,128)(2,1)} %gather_fusion.1), kind=kOutput, calls=%fused_computation.129.clone.1 | convolution fusion | flops 134217728 | bytes 5242880 | tf_op jit(solution)/shard_map/while/body/eval_jaxpr/krp,kps->ksr/dot_general | solution.py:110
  35.9 3.8 %scatter_fusion = f32[8,64,128]{2,1,0:T(8,128)S(1)} fusion(f32[8,64,128]{2,1,0:T(8,128)S(1)} %get-tuple-element.442, s32[64]{0:T(128)S(1)} %compare_select_fusion.10, f32[64,64,128]{2,1,0:T(8,128)S(1)} %fusion.79), kind=kCustom, calls=%fused_computation.4.clone.1 | custom fusion | flops 524288 | bytes 6291712 | tf_op jit(solution)/shard_map/while/body/eval_jaxpr/scatter-add | solution.py:116
  39.9 2.2 %gather_fusion = bf16[64,128,64]{2,1,0:T(8,128)(2,1)} fusion(bf16[16,128,64]{2,1,0:T(8,128)(2,1)S(1)} %get-tuple-element.456, s32[1024]{0:T(1024)S(1)} %pad_clamp_fusion.8), kind=kCustom, calls=%fused_computation.clone.1 | custom fusion | bytes 2097408 | tf_op jit(solution)/shard_map/while/body/eval_jaxpr/gather | solution.py:113
  42.0 2.1 %gather_fusion.1 = bf16[64,128,128]{2,1,0:T(8,128)(2,1)} fusion(bf16[16,128,128]{2,1,0:T(8,128)(2,1)S(1)} %get-tuple-element.458, s32[1024]{0:T(1024)S(1)} %pad_clamp_fusion.9), kind=kCustom, calls=%fused_computation.1.clone.1 | custom fusion | bytes 4194560 | tf_op jit(solution)/shard_map/while/body/eval_jaxpr/gather | solution.py:112
  44.1 3.7 %fusion.79 = f32[64,64,128]{2,1,0:T(8,128)S(1)} fusion(bf16[64,128,64]{2,1,0:T(8,128)(2,1)} %gather_fusion, bf16[64,128,128]{2,1,0:T(8,128)(2,1)} %gather_fusion.1), kind=kOutput, calls=%fused_computation.129.clone.1 | convolution fusion | flops 134217728 | bytes 5242880 | tf_op jit(solution)/shard_map/while/body/eval_jaxpr/krp,kps->ksr/dot_general | solution.py:110
  47.9 3.8 %scatter_fusion = f32[8,64,128]{2,1,0:T(8,128)S(1)} fusion(f32[8,64,128]{2,1,0:T(8,128)S(1)} %get-tuple-element.442, s32[64]{0:T(128)S(1)} %compare_select_fusion.10, f32[64,64,128]{2,1,0:T(8,128)S(1)} %fusion.79), kind=kCustom, calls=%fused_computation.4.clone.1 | custom fusion | flops 524288 | bytes 6291712 | tf_op jit(solution)/shard_map/while/body/eval_jaxpr/scatter-add | solution.py:116
  51.8 2.2 %gather_fusion = bf16[64,128,64]{2,1,0:T(8,128)(2,1)} fusion(bf16[16,128,64]{2,1,0:T(8,128)(2,1)S(1)} %get-tuple-element.456, s32[1024]{0:T(1024)S(1)} %pad_clamp_fusion.8), kind=kCustom, calls=%fused_computation.clone.1 | custom fusion | bytes 2097408 | tf_op jit(solution)/shard_map/while/body/eval_jaxpr/gather | solution.py:113
  54.0 2.1 %gather_fusion.1 = bf16[64,128,128]{2,1,0:T(8,128)(2,1)} fusion(bf16[16,128,128]{2,1,0:T(8,128)(2,1)S(1)} %get-tuple-element.458, s32[1024]{0:T(1024)S(1)} %pad_clamp_fusion.9), kind=kCustom, calls=%fused_computation.1.clone.1 | custom fusion | bytes 4194560 | tf_op jit(solution)/shard_map/while/body/eval_jaxpr/gather | solution.py:112
  56.1 3.7 %fusion.79 = f32[64,64,128]{2,1,0:T(8,128)S(1)} fusion(bf16[64,128,64]{2,1,0:T(8,128)(2,1)} %gather_fusion, bf16[64,128,128]{2,1,0:T(8,128)(2,1)} %gather_fusion.1), kind=kOutput, calls=%fused_computation.129.clone.1 | convolution fusion | flops 134217728 | bytes 5242880 | tf_op jit(solution)/shard_map/while/body/eval_jaxpr/krp,kps->ksr/dot_general | solution.py:110
  59.9 3.8 %scatter_fusion = f32[8,64,128]{2,1,0:T(8,128)S(1)} fusion(f32[8,64,128]{2,1,0:T(8,128)S(1)} %get-tuple-element.442, s32[64]{0:T(128)S(1)} %compare_select_fusion.10, f32[64,64,128]{2,1,0:T(8,128)S(1)} %fusion.79), kind=kCustom, calls=%fused_computation.4.clone.1 | custom fusion | flops 524288 | bytes 6291712 | tf_op jit(solution)/shard_map/while/body/eval_jaxpr/scatter-add | solution.py:116
  63.8 2.2 %gather_fusion = bf16[64,128,64]{2,1,0:T(8,128)(2,1)} fusion(bf16[16,128,64]{2,1,0:T(8,128)(2,1)S(1)} %get-tuple-element.456, s32[1024]{0:T(1024)S(1)} %pad_clamp_fusion.8), kind=kCustom, calls=%fused_computation.clone.1 | custom fusion | bytes 2097408 | tf_op jit(solution)/shard_map/while/body/eval_jaxpr/gather | solution.py:113
  66.0 2.1 %gather_fusion.1 = bf16[64,128,128]{2,1,0:T(8,128)(2,1)} fusion(bf16[16,128,128]{2,1,0:T(8,128)(2,1)S(1)} %get-tuple-element.458, s32[1024]{0:T(1024)S(1)} %pad_clamp_fusion.9), kind=kCustom, calls=%fused_computation.1.clone.1 | custom fusion | bytes 4194560 | tf_op jit(solution)/shard_map/while/body/eval_jaxpr/gather | solution.py:112
  68.1 3.7 %fusion.79 = f32[64,64,128]{2,1,0:T(8,128)S(1)} fusion(bf16[64,128,64]{2,1,0:T(8,128)(2,1)} %gather_fusion, bf16[64,128,128]{2,1,0:T(8,128)(2,1)} %gather_fusion.1), kind=kOutput, calls=%fused_computation.129.clone.1 | convolution fusion | flops 134217728 | bytes 5242880 | tf_op jit(solution)/shard_map/while/body/eval_jaxpr/krp,kps->ksr/dot_general | solution.py:110
  71.8 3.8 %scatter_fusion = f32[8,64,128]{2,1,0:T(8,128)S(1)} fusion(f32[8,64,128]{2,1,0:T(8,128)S(1)} %get-tuple-element.442, s32[64]{0:T(128)S(1)} %compare_select_fusion.10, f32[64,64,128]{2,1,0:T(8,128)S(1)} %fusion.79), kind=kCustom, calls=%fused_computation.4.clone.1 | custom fusion | flops 524288 | bytes 6291712 | tf_op jit(solution)/shard_map/while/body/eval_jaxpr/scatter-add | solution.py:116
  76.3 6.0 %all-to-all-start.2 = ((bf16[8,64,128]{2,1,0:T(8,128)(2,1)}), bf16[8,64,128]{2,1,0:T(8,128)(2,1)S(1)}, u32[]{:S(2)}, u32[]{:S(2)}) async-start(bf16[8,64,128]{2,1,0:T(8,128)(2,1)} %convert_element_type.108), calls=%async_computation.2 | async-start | bytes 262144 | tf_op jit(solution)/shard_map/all_to_all | solution.py:121
  84.2 4.8 %sort.16 = (f32[8,8,2048]{2,0,1:T(8,128)S(1)}, s32[8,8,2048]{2,0,1:T(8,128)}) sort(f32[8,8,2048]{2,0,1:T(8,128)S(1)} %copy_select_fusion, s32[8,8,2048]{2,0,1:T(8,128)S(1)} %iota.19), dimensions={0}, to_apply=%region_1.2 | sort | flops 2228224 | bytes 2097152 | tf_op jit(solution)/shard_map/jit(median)/jit(quantile)/sort | solution.py:54
  89.2 1.3 collective-permute-start.3
  90.5 4.1 %collective-permute-start.2 = (f32[8,8]{1,0:T(8,128)S(1)}, f32[8,8]{1,0:T(8,128)S(1)}, u32[]{:S(2)}, u32[]{:S(2)}) collective-permute-start(f32[8,8]{1,0:T(8,128)S(1)} %get-tuple-element.334), channel_id=1, source_target_pairs={{0,1},{1,2},{2,3},{4,5},{5,6},{6,7},{8,9},{9,10},{10,11},{12,13},{... | collective-permute-start | bytes 776 | tf_op jit(solution)/shard_map/ppermute | solution.py:18
  100.9 5.7 %all-to-all-start.1 = ((bf16[8,1,8,2048]{3,2,1,0:T(8,128)(2,1)}), bf16[8,1,8,2048]{3,2,1,0:T(8,128)(2,1)S(1)}, u32[]{:S(2)}, u32[]{:S(2)}) async-start(bf16[8,1,8,2048]{3,2,1,0:T(8,128)(2,1)} %fusion.42), calls=%async_computation.1 | async-start | bytes 524288 | tf_op jit(solution)/shard_map/all_to_all | solution.py:89
  106.9 8.1 %all-to-all-done.1 = bf16[8,1,8,2048]{3,2,1,0:T(8,128)(2,1)S(1)} async-done(((bf16[8,1,8,2048]{3,2,1,0:T(8,128)(2,1)}), bf16[8,1,8,2048]{3,2,1,0:T(8,128)(2,1)S(1)}, u32[]{:S(2)}, u32[]{:S(2)}) %all-to-all-start.1) | async-done | bytes 262176 | tf_op jit(solution)/shard_map/all_to_all | solution.py:89
  116.1 5.0 %all-to-all-start.3 = ((bf16[8,64,128]{2,1,0:T(8,128)(2,1)}), bf16[8,64,128]{2,1,0:T(8,128)(2,1)S(1)}, u32[]{:S(2)}, u32[]{:S(2)}) async-start(bf16[8,64,128]{2,1,0:T(8,128)(2,1)} %copy.47), calls=%async_computation.3 | async-start | bytes 262144 | tf_op jit(solution)/shard_map/all_to_all | solution.py:138
  121.1 7.4 %all-to-all-done.3 = bf16[8,64,128]{2,1,0:T(8,128)(2,1)S(1)} async-done(((bf16[8,64,128]{2,1,0:T(8,128)(2,1)}), bf16[8,64,128]{2,1,0:T(8,128)(2,1)S(1)}, u32[]{:S(2)}, u32[]{:S(2)}) %all-to-all-start.3) | async-done | bytes 131104 | tf_op jit(solution)/shard_map/all_to_all | solution.py:138
  128.6 41.5 %while.29 = (s32[]{:T(128)}, f32[16,128,64]{1,2,0:T(8,128)S(1)}, s32[256]{0:T(256)S(1)}, s32[256]{0:T(256)S(1)}, bf16[16,128,128]{2,1,0:T(8,128)(2,1)S(1)}, /*in...) while((s32[]{:T(128)}, f32[16,128,64]{1,2,0:T(8,128)S(1)}, ...), condition=%wide.region_7.8_spmd, body=%wide.region_5.7_spmd.sunk | while | flops 134744640 | bytes 17836972 | solution.py:150
  128.8 1.7 gather_fusion.2
  130.4 2.2 %gather_fusion.3 = bf16[64,128,128]{2,1,0:T(8,128)(2,1)} fusion(bf16[16,128,128]{2,1,0:T(8,128)(2,1)S(1)} %get-tuple-element.489, s32[1024]{0:T(1024)S(1)} %pad_clamp_fusion.11), kind=kCustom, calls=%fused_computation.2.clone.1 | custom fusion | bytes 4194560 | tf_op jit(solution)/shard_map/while/body/eval_jaxpr/gather | solution.py:146
  132.6 2.6 %fusion.82 = f32[64,128,64]{1,2,0:T(8,128)S(1)} fusion(bf16[64,64,128]{2,1,0:T(8,128)(2,1)} %gather_fusion.2, bf16[64,128,128]{2,1,0:T(8,128)(2,1)} %gather_fusion.3), kind=kOutput, calls=%fused_computation.130.clone.1 | convolution fusion | flops 134217728 | bytes 5242880 | tf_op jit(solution)/shard_map/while/body/eval_jaxpr/krp,ksr->kps/dot_general | solution.py:145
  135.2 3.7 %scatter_fusion.1 = f32[16,128,64]{1,2,0:T(8,128)S(1)} fusion(f32[16,128,64]{1,2,0:T(8,128)S(1)} %get-tuple-element.475, s32[64]{0:T(128)S(1)} %compare_select_fusion.12, f32[64,128,64]{1,2,0:T(8,128)S(1)} %fusion.82), kind=kCustom, calls=%fused_computation.5.clone.1 | custom fusion | flops 524288 | bytes 6291712 | tf_op jit(solution)/shard_map/while/body/eval_jaxpr/scatter-add | solution.py:148
  139.1 1.7 gather_fusion.2
  140.8 2.2 %gather_fusion.3 = bf16[64,128,128]{2,1,0:T(8,128)(2,1)} fusion(bf16[16,128,128]{2,1,0:T(8,128)(2,1)S(1)} %get-tuple-element.489, s32[1024]{0:T(1024)S(1)} %pad_clamp_fusion.11), kind=kCustom, calls=%fused_computation.2.clone.1 | custom fusion | bytes 4194560 | tf_op jit(solution)/shard_map/while/body/eval_jaxpr/gather | solution.py:146
  143.0 2.6 %fusion.82 = f32[64,128,64]{1,2,0:T(8,128)S(1)} fusion(bf16[64,64,128]{2,1,0:T(8,128)(2,1)} %gather_fusion.2, bf16[64,128,128]{2,1,0:T(8,128)(2,1)} %gather_fusion.3), kind=kOutput, calls=%fused_computation.130.clone.1 | convolution fusion | flops 134217728 | bytes 5242880 | tf_op jit(solution)/shard_map/while/body/eval_jaxpr/krp,ksr->kps/dot_general | solution.py:145
  145.5 3.8 %scatter_fusion.1 = f32[16,128,64]{1,2,0:T(8,128)S(1)} fusion(f32[16,128,64]{1,2,0:T(8,128)S(1)} %get-tuple-element.475, s32[64]{0:T(128)S(1)} %compare_select_fusion.12, f32[64,128,64]{1,2,0:T(8,128)S(1)} %fusion.82), kind=kCustom, calls=%fused_computation.5.clone.1 | custom fusion | flops 524288 | bytes 6291712 | tf_op jit(solution)/shard_map/while/body/eval_jaxpr/scatter-add | solution.py:148
  149.5 1.7 gather_fusion.2
  151.2 2.2 %gather_fusion.3 = bf16[64,128,128]{2,1,0:T(8,128)(2,1)} fusion(bf16[16,128,128]{2,1,0:T(8,128)(2,1)S(1)} %get-tuple-element.489, s32[1024]{0:T(1024)S(1)} %pad_clamp_fusion.11), kind=kCustom, calls=%fused_computation.2.clone.1 | custom fusion | bytes 4194560 | tf_op jit(solution)/shard_map/while/body/eval_jaxpr/gather | solution.py:146
  153.3 2.6 %fusion.82 = f32[64,128,64]{1,2,0:T(8,128)S(1)} fusion(bf16[64,64,128]{2,1,0:T(8,128)(2,1)} %gather_fusion.2, bf16[64,128,128]{2,1,0:T(8,128)(2,1)} %gather_fusion.3), kind=kOutput, calls=%fused_computation.130.clone.1 | convolution fusion | flops 134217728 | bytes 5242880 | tf_op jit(solution)/shard_map/while/body/eval_jaxpr/krp,ksr->kps/dot_general | solution.py:145
  155.9 3.8 %scatter_fusion.1 = f32[16,128,64]{1,2,0:T(8,128)S(1)} fusion(f32[16,128,64]{1,2,0:T(8,128)S(1)} %get-tuple-element.475, s32[64]{0:T(128)S(1)} %compare_select_fusion.12, f32[64,128,64]{1,2,0:T(8,128)S(1)} %fusion.82), kind=kCustom, calls=%fused_computation.5.clone.1 | custom fusion | flops 524288 | bytes 6291712 | tf_op jit(solution)/shard_map/while/body/eval_jaxpr/scatter-add | solution.py:148
  159.9 1.7 gather_fusion.2
  161.5 2.2 %gather_fusion.3 = bf16[64,128,128]{2,1,0:T(8,128)(2,1)} fusion(bf16[16,128,128]{2,1,0:T(8,128)(2,1)S(1)} %get-tuple-element.489, s32[1024]{0:T(1024)S(1)} %pad_clamp_fusion.11), kind=kCustom, calls=%fused_computation.2.clone.1 | custom fusion | bytes 4194560 | tf_op jit(solution)/shard_map/while/body/eval_jaxpr/gather | solution.py:146
  163.7 2.6 %fusion.82 = f32[64,128,64]{1,2,0:T(8,128)S(1)} fusion(bf16[64,64,128]{2,1,0:T(8,128)(2,1)} %gather_fusion.2, bf16[64,128,128]{2,1,0:T(8,128)(2,1)} %gather_fusion.3), kind=kOutput, calls=%fused_computation.130.clone.1 | convolution fusion | flops 134217728 | bytes 5242880 | tf_op jit(solution)/shard_map/while/body/eval_jaxpr/krp,ksr->kps/dot_general | solution.py:145
  166.3 3.8 %scatter_fusion.1 = f32[16,128,64]{1,2,0:T(8,128)S(1)} fusion(f32[16,128,64]{1,2,0:T(8,128)S(1)} %get-tuple-element.475, s32[64]{0:T(128)S(1)} %compare_select_fusion.12, f32[64,128,64]{1,2,0:T(8,128)S(1)} %fusion.82), kind=kCustom, calls=%fused_computation.5.clone.1 | custom fusion | flops 524288 | bytes 6291712 | tf_op jit(solution)/shard_map/while/body/eval_jaxpr/scatter-add | solution.py:148
  172.8 19.1 %reduce-scatter.2.cloned.1.call-done = f32[512,64]{0,1:T(8,128)} async-done(((f32[2048,64]{0,1:T(8,128)}), f32[512,64]{0,1:T(8,128)}) %reduce-scatter.2.cloned.1.call-update) | async-done | bytes 131088 | tf_op jit(solution)/shard_map/reduce_scatter | solution.py:155
  191.9 1.6 multiply_add_fusion
  (99 shorter events, 22.0 us)
Async XLA Ops:
  8.0 7.3 %collective-permute-start = (bf16[1,64,64]{2,1,0:T(8,128)(2,1)S(1)}, bf16[1,64,64]{2,1,0:T(8,128)(2,1)S(1)}, u32[]{:S(2)}, u32[]{:S(2)}) collective-permute-start(bf16[1,64,64]{2,1,0:T(8,128)(2,1)S(1)} %get-tuple-element.333), channel_id=1, source_target_pairs={{0,1},{1,2},{2,3},{4,5},{5,6},{6,7},{8,9},{9,10},{10,11},{12,13},{... | collective-permute-start | bytes 24584 | tf_op jit(solution)/shard_map/ppermute | solution.py:18
  10.4 5.2 %collective-permute-start.1 = (bf16[1,64,64]{2,1,0:T(8,128)(2,1)S(1)}, bf16[1,64,64]{2,1,0:T(8,128)(2,1)S(1)}, u32[]{:S(2)}, u32[]{:S(2)}) collective-permute-start(bf16[1,64,64]{2,1,0:T(8,128)(2,1)S(1)} %get-tuple-element.332), channel_id=1, source_target_pairs={{1,0},{2,1},{3,2},{5,4},{6,5},{7,6},{9,8},{10,9},{11,10},{13,12},{... | collective-permute-start | bytes 24584 | tf_op jit(solution)/shard_map/ppermute | solution.py:20
  17.1 10.6 %copy-start = (bf16[1,1,16,128,128]{4,3,2,1,0:T(8,128)(2,1)S(1)}, bf16[1,1,16,128,128]{4,3,2,1,0:T(8,128)(2,1)}, u32[]{:S(2)}) copy-start(bf16[1,1,16,128,128]{4,3,2,1,0:T(8,128)(2,1)} %param.16) | copy-start | bytes 1572868
  17.1 10.6 %copy-start.2 = (s32[1,1,256]{2,1,0:T(1,128)S(1)}, s32[1,1,256]{2,1,0:T(1,128)}, u32[]{:S(2)}) copy-start(s32[1,1,256]{2,1,0:T(1,128)} %param.17) | copy-start | bytes 3076
  17.1 10.6 %copy-start.3 = (s32[1,1,256]{2,1,0:T(1,128)S(1)}, s32[1,1,256]{2,1,0:T(1,128)}, u32[]{:S(2)}) copy-start(s32[1,1,256]{2,1,0:T(1,128)} %param.18) | copy-start | bytes 3076
  21.2 55.1 %all-to-all-start = ((bf16[8,2,8192]{2,1,0:T(2,128)(2,1)}), bf16[8,2,8192]{2,1,0:T(2,128)(2,1)}, u32[]{:S(2)}, u32[]{:S(2)}) async-start(bf16[8,2,8192]{2,1,0:T(2,128)(2,1)} %reshape.293), calls=%async_computation | async-start | bytes 524288 | tf_op jit(solution)/shard_map/all_to_all | solution.py:82
  76.3 24.6 %all-to-all-start.2 = ((bf16[8,64,128]{2,1,0:T(8,128)(2,1)}), bf16[8,64,128]{2,1,0:T(8,128)(2,1)S(1)}, u32[]{:S(2)}, u32[]{:S(2)}) async-start(bf16[8,64,128]{2,1,0:T(8,128)(2,1)} %convert_element_type.108), calls=%async_computation.2 | async-start | bytes 262144 | tf_op jit(solution)/shard_map/all_to_all | solution.py:121
  84.2 22.4 %copy-start.5 = (s32[1,1,8]{2,1,0:T(1,128)S(1)}, s32[1,1,8]{2,1,0:T(1,128)}, u32[]{:S(2)}) copy-start(s32[1,1,8]{2,1,0:T(1,128)} %param.21) | copy-start | bytes 100
  89.2 5.4 %collective-permute-start.3 = (f32[8,8]{1,0:T(8,128)S(1)}, f32[8,8]{1,0:T(8,128)S(1)}, u32[]{:S(2)}, u32[]{:S(2)}) collective-permute-start(f32[8,8]{1,0:T(8,128)S(1)} %get-tuple-element.335), channel_id=1, source_target_pairs={{1,0},{2,1},{3,2},{5,4},{6,5},{7,6},{9,8},{10,9},{11,10},{13,12},{... | collective-permute-start | bytes 776 | tf_op jit(solution)/shard_map/ppermute | solution.py:20
  90.5 4.9 %collective-permute-start.2 = (f32[8,8]{1,0:T(8,128)S(1)}, f32[8,8]{1,0:T(8,128)S(1)}, u32[]{:S(2)}, u32[]{:S(2)}) collective-permute-start(f32[8,8]{1,0:T(8,128)S(1)} %get-tuple-element.334), channel_id=1, source_target_pairs={{0,1},{1,2},{2,3},{4,5},{5,6},{6,7},{8,9},{9,10},{10,11},{12,13},{... | collective-permute-start | bytes 776 | tf_op jit(solution)/shard_map/ppermute | solution.py:18
  100.9 14.2 %all-to-all-start.1 = ((bf16[8,1,8,2048]{3,2,1,0:T(8,128)(2,1)}), bf16[8,1,8,2048]{3,2,1,0:T(8,128)(2,1)S(1)}, u32[]{:S(2)}, u32[]{:S(2)}) async-start(bf16[8,1,8,2048]{3,2,1,0:T(8,128)(2,1)} %fusion.42), calls=%async_computation.1 | async-start | bytes 524288 | tf_op jit(solution)/shard_map/all_to_all | solution.py:89
  106.9 9.2 %copy-start.1 = (f32[1,64,16,128]{3,2,1,0:T(8,128)}, f32[1,64,16,128]{3,2,1,0:T(8,128)S(1)}, u32[]{:S(2)}) copy-start(f32[1,64,16,128]{3,2,1,0:T(8,128)S(1)} %convolution_bitcast_fusion) | copy-start | bytes 1572868
  106.9 21.7 %copy-start.4 = (s32[1,1,256]{2,1,0:T(1,128)S(1)}, s32[1,1,256]{2,1,0:T(1,128)}, u32[]{:S(2)}) copy-start(s32[1,1,256]{2,1,0:T(1,128)} %param.19) | copy-start | bytes 3076
  116.1 12.5 %all-to-all-start.3 = ((bf16[8,64,128]{2,1,0:T(8,128)(2,1)}), bf16[8,64,128]{2,1,0:T(8,128)(2,1)S(1)}, u32[]{:S(2)}, u32[]{:S(2)}) async-start(bf16[8,64,128]{2,1,0:T(8,128)(2,1)} %copy.47), calls=%async_computation.3 | async-start | bytes 262144 | tf_op jit(solution)/shard_map/all_to_all | solution.py:138
  121.1 70.9 %reduce-scatter.2.cloned.1.call-start = ((), (), s32[]{:S(2)}) async-start(), calls=%async_computation.5 | async-start | bytes 655360 | tf_op jit(solution)/shard_map/reduce_scatter | solution.py:155
Sparse Core Ops, SparseCore 0:
  171.1 20.8 reduce-scatter.1
